TPU v7x, 32 devices: a whole 2x2x4 slice. The times are simulated.
32 devices in a mesh: blk: 16 (over z, x, core), cuts: 2 (over y).
Axes of the slice: x: 2, y: 2, z: 4, core: 2. Of those that a mesh axis runs over, the one named last changes fastest.
Arguments:
- left_env: bfloat16 [2048, 8, 2048], P('blk', 'cuts'), may hold values from -4 to 4
- right_env: bfloat16 [2048, 8, 2048], P('blk', 'cuts'), may hold values from -4 to 4
- left_core: float32 [8, 8, 2, 2], replicated, may hold values from -1.5 to 1.5
- right_core: float32 [8, 8, 2, 2], replicated, may hold values from -1.5 to 1.5
- slot_bond: int32 [8], replicated, may hold values from 0 to 7, each once
- krylov_basis: float32 [8, 2048, 4, 2048], P(None, 'blk', None, 'cuts'), may hold values from -30 to 30
- beta_prev: float32 [], replicated, may hold values from 0.3 to 1.2
Outputs:
- next_vector: float32 [2048, 4, 2048], P('blk', None, 'cuts')
- alpha_values: float32 [1], replicated
- beta_values: float32 [1], replicated
Inputs may be any that keep to these rules, and one draw needn't show every extreme that they name: `slot_bond`: a permutation of the 8 bond values.
All inputs are finite; a program needn't handle non-finite values.
Results may differ from a plain program's by a relative error of at most 0.00073.
The roundings to bfloat16 on the way count: a program that leaves them out, or rounds other values in their place, can miss the bound.
Values may be sent and summed in bfloat16 or wider, within the bound.
A program may use at most 192 MiB of HBM per device.

v0:
```python
import jax
import jax.numpy as jnp
from jax import lax
from jax.sharding import PartitionSpec as P


def build_table(left_core, right_core, slot_bond):
    bond_width = left_core.shape[0]
    phys_dim = left_core.shape[2]
    chosen = (slot_bond[:, None] == jnp.arange(bond_width, dtype=jnp.int32)[None, :]).astype(
        jnp.float32
    )
    picked = jnp.einsum("kw,wxac->kxac", chosen, left_core, precision=lax.Precision.HIGHEST)
    table = jnp.einsum("kxac,xybd->kyabcd", picked, right_core, precision=lax.Precision.HIGHEST)
    return table.reshape(bond_width, bond_width, phys_dim * phys_dim, phys_dim * phys_dim)


def on_device(left_env, right_env, left_core, right_core, slot_bond, krylov_basis, beta_prev):
    highest = lax.Precision.HIGHEST
    bond_width = left_core.shape[0]
    pair_count = left_core.shape[2] * left_core.shape[2]
    basis_count = krylov_basis.shape[0]
    row_count = krylov_basis.shape[1]
    col_count = krylov_basis.shape[3]
    full_width = left_env.shape[2]
    entries = float(full_width * pair_count * full_width)
    mpo_table = build_table(left_core, right_core, slot_bond)
    left_full = lax.all_gather(left_env, "cuts", axis=1, tiled=True)
    left_matrix = left_full.reshape(row_count * bond_width, full_width)
    right_local = lax.all_to_all(right_env, "cuts", split_axis=2, concat_axis=1, tiled=True)
    next_vector = krylov_basis[basis_count - 1]
    current_f = krylov_basis[basis_count - 1]
    previous = krylov_basis[basis_count - 2]
    current = current_f.astype(jnp.bfloat16)
    block_rows = lax.all_gather(current, "blk", axis=0, tiled=True)
    count_rows = block_rows.shape[0]
    projected = jnp.dot(
        left_matrix,
        block_rows.reshape(count_rows, pair_count * col_count),
        preferred_element_type=jnp.float32,
    )
    projected = projected.reshape(row_count, bond_width, pair_count, col_count)
    mixed_left = jnp.einsum("kypq,akqb->apyb", mpo_table, projected, precision=highest).astype(
        jnp.bfloat16
    )
    left_side = mixed_left.reshape(row_count * pair_count, bond_width * col_count)
    block_rows = lax.all_gather(right_local, "blk", axis=0, tiled=True)
    flat_rows = block_rows.reshape(block_rows.shape[0], -1)
    partial_terms = lax.dot_general(
        left_side, flat_rows, (((1,), (1,)), ((), ())), preferred_element_type=jnp.float32
    )
    image_vec = lax.psum_scatter(
        partial_terms.reshape(row_count, pair_count, full_width),
        "cuts",
        scatter_dimension=2,
        tiled=True,
    )
    local_gram = jnp.einsum("japb,kapb->jk", krylov_basis, krylov_basis, precision=highest)
    gram_matrix = lax.psum(local_gram, ("blk", "cuts")) / entries
    local_prods = jnp.einsum("japb,apb->j", krylov_basis, image_vec, precision=highest)
    inner_prods, image_square = lax.psum(
        (local_prods, jnp.sum(image_vec * image_vec)), ("blk", "cuts")
    )
    inner_prods = inner_prods / entries
    image_square = image_square / entries
    alpha_now = inner_prods[basis_count - 1]
    ortho_coeffs = (
        inner_prods
        - alpha_now * gram_matrix[:, basis_count - 1]
        - beta_prev * gram_matrix[:, basis_count - 2]
    )
    first_square = (
        image_square
        - 2.0 * alpha_now * inner_prods[basis_count - 1]
        - 2.0 * beta_prev * inner_prods[basis_count - 2]
        + alpha_now * alpha_now * gram_matrix[basis_count - 1, basis_count - 1]
        + 2.0 * alpha_now * beta_prev * gram_matrix[basis_count - 1, basis_count - 2]
        + beta_prev * beta_prev * gram_matrix[basis_count - 2, basis_count - 2]
    )
    square_mean = (
        first_square
        - 2.0 * jnp.sum(ortho_coeffs * ortho_coeffs)
        + jnp.sum(ortho_coeffs[:, None] * gram_matrix * ortho_coeffs[None, :])
    )
    first_pass = image_vec - alpha_now * current_f - beta_prev * previous
    second_pass = first_pass - jnp.einsum(
        "j,japb->apb", ortho_coeffs, krylov_basis, precision=highest
    )
    beta_new = jnp.sqrt(square_mean + 1e-06)
    next_vector = second_pass / beta_new
    alpha_list = [alpha_now]
    beta_list = [beta_new]
    return (next_vector, jnp.stack(alpha_list), jnp.stack(beta_list))


def solution(mesh):
    in_specs = (
        P("blk", "cuts", None),
        P("blk", "cuts", None),
        P(),
        P(),
        P(),
        P(None, "blk", None, "cuts"),
        P(),
    )
    out_specs = (P("blk", None, "cuts"), P(), P())
    return jax.shard_map(
        on_device, mesh=mesh, in_specs=in_specs, out_specs=out_specs, check_vma=False
    )
```

profile of v0, /device:TPU:0, one launch (start us, length us, event | category | flops | bytes accessed | tf_op | source)
XLA Modules:
  0.0 616.2 jit_solution(4557364010513093199)
XLA Ops:
  7.2 0.0 copy-start
  7.2 0.0 all-gather.9.cloned.1.call-start
  7.2 4.5 fusion.43
  11.7 0.0 copy-start.3
  11.7 0.0 copy-start.4
  11.7 1.3 copy-done.3
  13.1 2.1 copy.113
  15.2 0.0 all-gather.9.cloned.1.call-update
  15.2 0.0 all-gather.5.cloned.1.call-start
  15.2 0.0 copy-done.4
  15.2 2.5 copy.42
  17.7 0.0 all-gather.5.cloned.1.call-update
  17.8 0.0 all-gather.7.cloned.1.call-start
  17.8 5.6 copy.50
  23.4 30.2 %all_to_all.18 = bf16[128,4,2048]{0,1,2:T(4,128)(2,1)S(1)} all-to-all(bf16[128,4,2048]{0,1,2:T(4,128)(2,1)} %copy.50), channel_id=1, replica_groups=mesh['blk'=16,'cuts'=2] {'cuts'}, dimensions={2} | all-to-all | bytes 4194304 | tf_op jit(solution)/shard_map/all_to_all | solution.py:30
  53.6 0.0 copy-start.6
  53.6 0.0 copy-start.7
  53.6 2.7 copy.51
  56.3 0.0 all-gather.7.cloned.1.call-update
  56.3 0.0 reduce-scatter.2.cloned.1.call-start
  56.3 0.0 copy-done.6
  56.3 0.0 copy-done.7
  56.4 0.2 convolution_bitcast_fusion.1
  56.5 0.0 copy-done
  56.5 0.2 convolution_bitcast_fusion
  56.7 0.6 copy.48
  57.4 87.1 %all-gather.9.cloned.1.call-done = bf16[1,2048,4,1024]{3,1,2,0:T(8,128)(2,1)} async-done(((bf16[1,128,4,1024]{3,1,2,0:T(8,128)(2,1)}), bf16[1,2048,4,1024]{3,1,2,0:T(8,128)(2,1)}) %all-gather.9.cloned.1.call-update) | async-done | bytes 16777232 | tf_op jit(solution)/shard_map/all_gather | solution.py:35
  144.5 22.2 %copy.44 = bf16[1,2048,4,1024]{1,3,2,0:T(8,128)(2,1)} copy(bf16[1,2048,4,1024]{3,1,2,0:T(8,128)(2,1)} %all-gather.9.cloned.1.call-done) | data formatting | bytes 33554432 | tf_op jit(solution)/shard_map/all_gather | solution.py:35
  166.7 34.2 %all-gather.5.cloned.1.call-done = bf16[128,8,2048]{2,0,1:T(8,128)(2,1)} async-done(((bf16[128,4,2048]{2,0,1:T(8,128)(2,1)}), bf16[128,8,2048]{2,0,1:T(8,128)(2,1)}) %all-gather.5.cloned.1.call-update) | async-done | bytes 4194320 | tf_op jit(solution)/shard_map/all_gather | solution.py:28
  201.0 0.0 copy-start.5
  201.0 25.6 %fusion.4 = f32[128,8,4,1024]{3,1,2,0:T(8,128)} fusion(bf16[1,2048,4,1024]{1,3,2,0:T(8,128)(2,1)} %copy.44, bf16[128,8,2048,1]{2,0,1,3:T(8,128)(2,1)} %bitcast.94), kind=kOutput, calls=%fused_computation.4 | convolution fusion | flops 17179869184 | bytes 37748736 | tf_op jit(solution)/shard_map/dot_general | solution.py:37
  226.6 0.0 copy-done.5
  226.6 20.6 %fusion.15 = bf16[128,4,8,1024]{3,2,1,0:T(8,128)(2,1)} fusion(f32[8,8,4,4,1]{1,0,3,2,4:T(8,128)S(1)} %bitcast.93, f32[128,8,4,1024]{3,1,2,0:T(8,128)} %fusion.4), kind=kOutput, calls=%fused_computation.14 | convolution fusion | flops 1614807040 | bytes 25169920 | tf_op jit(solution)/shard_map/kypq,akqb->apyb/dot_general | solution.py:43
  247.2 123.4 %all-gather.7.cloned.1.call-done = bf16[2048,8,1024]{2,0,1:T(8,128)(2,1)} async-done(((bf16[128,8,1024]{2,0,1:T(8,128)(2,1)}), bf16[2048,8,1024]{2,0,1:T(8,128)(2,1)}) %all-gather.7.cloned.1.call-update) | async-done | bytes 33554448 | tf_op jit(solution)/shard_map/all_gather | solution.py:47
  370.6 46.7 %fusion.19 = f32[128,4,2048]{2,0,1:T(8,128)} fusion(bf16[2048,8,1024]{2,0,1:T(8,128)(2,1)} %all-gather.7.cloned.1.call-done, bf16[128,4,8,1024]{3,2,1,0:T(8,128)(2,1)} %fusion.15), kind=kOutput, calls=%fused_computation.16 | convolution fusion | flops 17179869184 | bytes 46137344 | tf_op jit(solution)/shard_map/dot_general | solution.py:49
  417.3 0.0 reduce-scatter.2.cloned.1.call-update
  418.0 54.5 %fusion.29 = f32[8,8]{1,0:T(8,128)S(1)} fusion(f32[8,128,4,1024]{3,2,1,0:T(4,128)} %param.12), kind=kOutput, calls=%fused_computation.28 | convolution fusion | flops 402653184 | bytes 16777472 | tf_op jit(solution)/shard_map/japb,kapb->jk/dot_general | solution.py:58
  472.5 0.0 reduce-scatter.2.cloned.1.call-done
  472.5 0.0 copy-start.2
  472.5 43.3 %fusion.32 = f32[8]{0:T(128)S(1)} fusion(f32[8,128,4,1024]{3,2,1,0:T(4,128)} %param.12, f32[128,4,1024,1]{2,0,1,3:T(8,128)} %bitcast.90), kind=kOutput, calls=%fused_computation.29 | convolution fusion | flops 50331648 | bytes 18874400 | tf_op jit(solution)/shard_map/japb,apb->j/dot_general | solution.py:60
  515.8 0.0 copy-done.2
  515.8 1.1 multiply_reduce_fusion
  517.0 39.9 %all-reduce = (f32[8,8]{1,0:T(8,128)S(1)}, f32[8]{0:T(128)S(1)}, f32[]{:T(128)}) all-reduce(f32[8,8]{1,0:T(8,128)S(1)} %fusion.29, f32[8]{0:T(128)S(1)} %fusion.32, f32[]{:T(128)} %multiply_reduce_fusion), channel_id=1, replica_groups=mesh['blk'=16,'cuts'=2] {'blk','cuts'}, use_global_device_ids=true, to_apply=%region_2.0 | all-reduce | flops 73 | bytes 584 | tf_op jit(solution)/shard_map/psum | solution.py:59
  556.9 0.6 fusion.45
  559.5 0.9 multiply_reduce_fusion.3
  560.3 0.7 fusion.44
  561.7 0.7 multiply_reduce_fusion.4
  562.3 30.8 %fusion.6 = f32[1,128,4,1024]{3,0,2,1:T(1,128)} fusion(f32[8,128,4,1024]{3,2,1,0:T(4,128)} %param.12, f32[8]{0:T(128)S(1)} %get-tuple-element.21), kind=kOutput, calls=%fused_computation.7 | convolution fusion | flops 50331648 | bytes 18874400 | tf_op jit(solution)/shard_map/j,japb->apb/dot_general | solution.py:86
  593.1 0.7 multiply_reduce_fusion.1
  598.4 0.0 copy-start.1
  598.4 6.9 %fusion.27 = f32[128,4,1024]{2,0,1:T(8,128)S(1)} fusion(f32[1,128,4,1024]{3,2,1,0:T(4,128)} %get-tuple-element.23, f32[128,4,1024]{2,0,1:T(8,128)S(1)} %copy-done.2, f32[1,128,4,1024]{3,0,2,1:T(1,128)} %fusion.6, f32[1,128,4,1024]{3,2,1,0:T(4,128)} %copy-done.3, f32[]{:T(128)} %sqrt.3, f32[]{:T(128)S(6)} %copy.114, f32[]{:T(128)} %bitcast.27), kind=kLoop, calls=%fused_computation.21 | loop fusion | flops 3145728 | bytes 10485772 | tf_op jit(solution)/shard_map/div | solution.py:90
  605.3 2.7 copy.56
  608.0 0.0 copy-done.1
  (3 shorter events, 0.0 us)
Async XLA Ops:
  7.2 49.4 %copy-start = (f32[8,8,2,2]{1,3,2,0:T(2,128)S(1)}, f32[8,8,2,2]{1,3,2,0:T(2,128)}, u32[]{:S(2)}) copy-start(f32[8,8,2,2]{1,3,2,0:T(2,128)} %param.10) | copy-start | bytes 3076
  7.2 137.3 %all-gather.9.cloned.1.call-start = ((), (), s32[]{:S(2)}) async-start(), calls=%async_computation.5 | async-start | bytes 17825792 | tf_op jit(solution)/shard_map/all_gather | solution.py:35
  11.7 1.3 copy-start.3
  11.7 3.5 copy-start.4
  15.2 185.8 %all-gather.5.cloned.1.call-start = ((), (), s32[]{:S(2)}) async-start(), calls=%async_computation.2 | async-start | bytes 6291456 | tf_op jit(solution)/shard_map/all_gather | solution.py:28
  17.8 352.9 %all-gather.7.cloned.1.call-start = ((), (), s32[]{:S(2)}) async-start(), calls=%async_computation.3 | async-start | bytes 35651584 | tf_op jit(solution)/shard_map/all_gather | solution.py:47
  53.6 2.8 copy-start.6
  53.6 2.8 copy-start.7
  56.3 416.2 %reduce-scatter.2.cloned.1.call-start = ((), (), s32[]{:S(2)}) async-start(), calls=%async_computation.4 | async-start | bytes 6291456 | tf_op jit(solution)/shard_map/reduce_scatter | solution.py:52
  201.0 25.6 %copy-start.5 = (f32[8,8,2,2,2,2]{1,0,5,4,3,2:T(8,128)S(1)}, f32[8,8,2,2,2,2]{1,0,5,4,3,2:T(8,128)}, u32[]{:S(2)}) copy-start(f32[8,8,2,2,2,2]{1,0,5,4,3,2:T(8,128)} %copy.48) | copy-start | bytes 12292
  472.5 43.3 %copy-start.2 = (f32[128,4,1024]{2,0,1:T(8,128)S(1)}, f32[128,4,1024]{2,0,1:T(8,128)}, u32[]{:S(2)}) copy-start(f32[128,4,1024]{2,0,1:T(8,128)} %reduce-scatter.2.cloned.1.call-done) | copy-start | bytes 6291460
  598.4 9.6 %copy-start.1 = (f32[8,8,2,2]{1,3,2,0:T(2,128)S(1)}, f32[8,8,2,2]{1,3,2,0:T(2,128)}, u32[]{:S(2)}) copy-start(f32[8,8,2,2]{1,3,2,0:T(2,128)} %param.10) | copy-start | bytes 3076
Sparse Core Ops, SparseCore 0:
  15.3 129.1 all-gather.8
  146.0 54.8 all-gather.4
  202.5 168.0 all-gather.6
  417.5 54.3 reduce-scatter.1
where the time goes:
time: 624 us; the launch traced here: 616 us
  waiting for transfers between devices  245 us (39%)
  matrix products  222 us (36%)
  blocking collectives  70.1 us (11%)
  local copies, waits for them, and re-layouts  45.5 us (7%)
  between operations  23.3 us (4%)
  other arithmetic  10.3 us (2%)
    all_gather x1, waiting for transfers between devices, on_device(): block_rows = lax.all_gather(right_local, 'blk', axis=0, tiled=True)  123 us
    all_gather x1, waiting for transfers between devices, on_device(): block_rows = lax.all_gather(current, 'blk', axis=0, tiled=True)  87.1 us
    dot_general x1, matrix products, on_device(): jnp.einsum('japb,kapb->jk', krylov_basis, krylov_basis, precision=highest)  54.5 us
    dot_general x1, matrix products, on_device(): lax.dot_general(left_side, flat_rows, (((1,), (1,)), ((), ())), preferred...  46.7 us
    dot_general x1, matrix products, on_device(): jnp.einsum('japb,apb->j', krylov_basis, image_vec, precision=highest)  43.3 us
    psum x1, blocking collectives, on_device(): gram_matrix = lax.psum(local_gram, ('blk', 'cuts')) / entries  39.9 us
    all_gather x1, waiting for transfers between devices, on_device(): left_full = lax.all_gather(left_env, 'cuts', axis=1, tiled=True)  34.2 us
    dot_general x1, matrix products, on_device(): jnp.einsum('j,japb->apb', ortho_coeffs, krylov_basis, precision=highest)  30.8 us
  transfers between devices with their start and end apart: 4, of which 3 were waited for; matrix products, arithmetic and copies ran while one was open for 22% of the time, Pallas kernels for 0%

commit v1 on v0

--- a/solution.py
+++ b/solution.py
@@ -56,7 +56,7 @@
         tiled=True,
     )
     local_gram = jnp.einsum("japb,kapb->jk", krylov_basis, krylov_basis, precision=highest)
-    gram_matrix = lax.psum(local_gram, ("blk", "cuts")) / entries
+    gram_matrix = lax.psum(lax.psum(local_gram, "cuts"), "blk") / entries
     local_prods = jnp.einsum("japb,apb->j", krylov_basis, image_vec, precision=highest)
     inner_prods, image_square = lax.psum(
         (local_prods, jnp.sum(image_vec * image_vec)), ("blk", "cuts")

time: 624 us -> 658 us (1.054)
  blocking collectives: 70.1 us -> 104 us
    psum x1 -> x3, blocking collectives: 39.9 us -> 73.5 us  [the longest x1 37.1 us: on_device(): lax.psum((local_prods, jnp.sum(image_vec * image_vec)), ('blk', 'cuts'))]
  transfers between devices with their start and end apart: 4 -> 4, of which waited for: 3 -> 3; matrix products, arithmetic and copies ran while one was open for 22% -> 21% of each run, Pallas kernels for 0% -> 0%
where the time goes in v1:
time: 658 us; the launch traced here: 649 us
  waiting for transfers between devices  245 us (37%)
  matrix products  222 us (34%)
  blocking collectives  104 us (16%)
  local copies, waits for them, and re-layouts  45.5 us (7%)
  between operations  22.7 us (3%)
  other arithmetic  10.2 us (2%)
    all_gather x1, waiting for transfers between devices, on_device(): block_rows = lax.all_gather(right_local, 'blk', axis=0, tiled=True)  123 us
    all_gather x1, waiting for transfers between devices, on_device(): block_rows = lax.all_gather(current, 'blk', axis=0, tiled=True)  87.1 us
    dot_general x1, matrix products, on_device(): jnp.einsum('japb,kapb->jk', krylov_basis, krylov_basis, precision=highest)  54.5 us
    dot_general x1, matrix products, on_device(): lax.dot_general(left_side, flat_rows, (((1,), (1,)), ((), ())), preferred...  46.7 us
    dot_general x1, matrix products, on_device(): jnp.einsum('japb,apb->j', krylov_basis, image_vec, precision=highest)  43.3 us
    psum x1, blocking collectives, on_device(): lax.psum((local_prods, jnp.sum(image_vec * image_vec)), ('blk', 'cuts'))  37.1 us
    psum x2, blocking collectives, on_device(): gram_matrix = lax.psum(lax.psum(local_gram, 'cuts'), 'blk') / entries  36.4 us
    all_gather x1, waiting for transfers between devices, on_device(): left_full = lax.all_gather(left_env, 'cuts', axis=1, tiled=True)  34.2 us
  transfers between devices with their start and end apart: 4, of which 3 were waited for; matrix products, arithmetic and copies ran while one was open for 21% of the time, Pallas kernels for 0%

profile of v1, /device:TPU:0, one launch (start us, length us, event | category | flops | bytes accessed | tf_op | source)
XLA Modules:
  0.0 649.1 jit_solution(1449605377218737297)
XLA Ops:
  7.2 0.0 copy-start
  7.2 0.0 all-gather.9.cloned.1.call-start
  7.2 4.5 fusion.43
  11.7 0.0 copy-start.3
  11.7 0.0 copy-start.4
  11.7 1.3 copy-done.3
  13.1 2.1 copy.113
  15.2 0.0 all-gather.9.cloned.1.call-update
  15.2 0.0 all-gather.5.cloned.1.call-start
  15.3 0.0 copy-done.4
  15.3 2.5 copy.42
  17.8 0.0 all-gather.5.cloned.1.call-update
  17.8 0.0 all-gather.7.cloned.1.call-start
  17.9 5.6 copy.50
  23.4 30.2 %all_to_all.18 = bf16[128,4,2048]{0,1,2:T(4,128)(2,1)S(1)} all-to-all(bf16[128,4,2048]{0,1,2:T(4,128)(2,1)} %copy.50), channel_id=1, replica_groups=mesh['blk'=16,'cuts'=2] {'cuts'}, dimensions={2} | all-to-all | bytes 4194304 | tf_op jit(solution)/shard_map/all_to_all | solution.py:30
  53.6 0.0 copy-start.6
  53.6 0.0 copy-start.7
  53.6 2.7 copy.51
  56.3 0.0 all-gather.7.cloned.1.call-update
  56.3 0.0 reduce-scatter.2.cloned.1.call-start
  56.4 0.0 copy-done.6
  56.4 0.0 copy-done.7
  56.4 0.2 convolution_bitcast_fusion.1
  56.6 0.0 copy-done
  56.6 0.2 convolution_bitcast_fusion
  56.8 0.6 copy.48
  57.4 87.1 %all-gather.9.cloned.1.call-done = bf16[1,2048,4,1024]{3,1,2,0:T(8,128)(2,1)} async-done(((bf16[1,128,4,1024]{3,1,2,0:T(8,128)(2,1)}), bf16[1,2048,4,1024]{3,1,2,0:T(8,128)(2,1)}) %all-gather.9.cloned.1.call-update) | async-done | bytes 16777232 | tf_op jit(solution)/shard_map/all_gather | solution.py:35
  144.5 22.2 %copy.44 = bf16[1,2048,4,1024]{1,3,2,0:T(8,128)(2,1)} copy(bf16[1,2048,4,1024]{3,1,2,0:T(8,128)(2,1)} %all-gather.9.cloned.1.call-done) | data formatting | bytes 33554432 | tf_op jit(solution)/shard_map/all_gather | solution.py:35
  166.8 34.2 %all-gather.5.cloned.1.call-done = bf16[128,8,2048]{2,0,1:T(8,128)(2,1)} async-done(((bf16[128,4,2048]{2,0,1:T(8,128)(2,1)}), bf16[128,8,2048]{2,0,1:T(8,128)(2,1)}) %all-gather.5.cloned.1.call-update) | async-done | bytes 4194320 | tf_op jit(solution)/shard_map/all_gather | solution.py:28
  201.0 0.0 copy-start.5
  201.0 25.6 %fusion.4 = f32[128,8,4,1024]{3,1,2,0:T(8,128)} fusion(bf16[1,2048,4,1024]{1,3,2,0:T(8,128)(2,1)} %copy.44, bf16[128,8,2048,1]{2,0,1,3:T(8,128)(2,1)} %bitcast.94), kind=kOutput, calls=%fused_computation.4 | convolution fusion | flops 17179869184 | bytes 37748736 | tf_op jit(solution)/shard_map/dot_general | solution.py:37
  226.6 0.0 copy-done.5
  226.6 20.7 %fusion.15 = bf16[128,4,8,1024]{3,2,1,0:T(8,128)(2,1)} fusion(f32[8,8,4,4,1]{1,0,3,2,4:T(8,128)S(1)} %bitcast.93, f32[128,8,4,1024]{3,1,2,0:T(8,128)} %fusion.4), kind=kOutput, calls=%fused_computation.14 | convolution fusion | flops 1614807040 | bytes 25169920 | tf_op jit(solution)/shard_map/kypq,akqb->apyb/dot_general | solution.py:43
  247.3 123.3 %all-gather.7.cloned.1.call-done = bf16[2048,8,1024]{2,0,1:T(8,128)(2,1)} async-done(((bf16[128,8,1024]{2,0,1:T(8,128)(2,1)}), bf16[2048,8,1024]{2,0,1:T(8,128)(2,1)}) %all-gather.7.cloned.1.call-update) | async-done | bytes 33554448 | tf_op jit(solution)/shard_map/all_gather | solution.py:47
  370.6 46.7 %fusion.19 = f32[128,4,2048]{2,0,1:T(8,128)} fusion(bf16[2048,8,1024]{2,0,1:T(8,128)(2,1)} %all-gather.7.cloned.1.call-done, bf16[128,4,8,1024]{3,2,1,0:T(8,128)(2,1)} %fusion.15), kind=kOutput, calls=%fused_computation.16 | convolution fusion | flops 17179869184 | bytes 46137344 | tf_op jit(solution)/shard_map/dot_general | solution.py:49
  417.3 0.0 reduce-scatter.2.cloned.1.call-update
  418.0 54.5 %fusion.29 = f32[8,8]{1,0:T(8,128)S(1)} fusion(f32[8,128,4,1024]{3,2,1,0:T(4,128)} %param.12), kind=kOutput, calls=%fused_computation.28 | convolution fusion | flops 402653184 | bytes 16777472 | tf_op jit(solution)/shard_map/japb,kapb->jk/dot_general | solution.py:58
  472.5 4.9 psum.29
  477.4 31.5 %psum.30 = f32[8,8]{1,0:T(8,128)S(1)} all-reduce(f32[8,8]{1,0:T(8,128)S(1)} %psum.29), channel_id=1, replica_groups=mesh['blk'=16,'cuts'=2] {'blk'}, use_global_device_ids=true, to_apply=%region_3.0 | all-reduce | flops 64 | bytes 512 | tf_op jit(solution)/shard_map/psum | solution.py:59
  508.9 0.6 fusion.44
  509.5 0.0 reduce-scatter.2.cloned.1.call-done
  509.5 0.0 copy-start.2
  509.5 43.3 %fusion.32 = f32[8]{0:T(128)S(1)} fusion(f32[8,128,4,1024]{3,2,1,0:T(4,128)} %param.12, f32[128,4,1024,1]{2,0,1,3:T(8,128)} %bitcast.90), kind=kOutput, calls=%fused_computation.29 | convolution fusion | flops 50331648 | bytes 18874400 | tf_op jit(solution)/shard_map/japb,apb->j/dot_general | solution.py:60
  552.8 0.0 copy-done.2
  552.8 1.1 multiply_reduce_fusion
  554.6 37.1 %all-reduce = (f32[8]{0:T(128)S(1)}, f32[]{:T(128)}) all-reduce(f32[8]{0:T(128)S(1)} %fusion.32, f32[]{:T(128)} %multiply_reduce_fusion), channel_id=1, replica_groups=mesh['blk'=16,'cuts'=2] {'blk','cuts'}, use_global_device_ids=true, to_apply=%region_1.0 | all-reduce | flops 9 | bytes 72 | tf_op jit(solution)/shard_map/psum | solution.py:61
  591.7 0.6 fusion.45
  592.3 0.9 multiply_reduce_fusion.3
  595.8 0.7 multiply_reduce_fusion.4
  596.4 30.9 %fusion.6 = f32[1,128,4,1024]{3,0,2,1:T(1,128)} fusion(f32[8,128,4,1024]{3,2,1,0:T(4,128)} %param.12, f32[8]{0:T(128)S(1)} %get-tuple-element.20), kind=kOutput, calls=%fused_computation.7 | convolution fusion | flops 50331648 | bytes 18874400 | tf_op jit(solution)/shard_map/j,japb->apb/dot_general | solution.py:86
  627.4 0.6 multiply_reduce_fusion.1
  631.7 0.0 copy-start.1
  631.7 6.9 %fusion.27 = f32[128,4,1024]{2,0,1:T(8,128)S(1)} fusion(f32[1,128,4,1024]{3,2,1,0:T(4,128)} %get-tuple-element.22, f32[128,4,1024]{2,0,1:T(8,128)S(1)} %copy-done.2, f32[1,128,4,1024]{3,0,2,1:T(1,128)} %fusion.6, f32[1,128,4,1024]{3,2,1,0:T(4,128)} %copy-done.3, f32[]{:T(128)} %sqrt.3, f32[]{:T(128)S(6)} %copy.114, f32[]{:T(128)} %bitcast.27), kind=kLoop, calls=%fused_computation.21 | loop fusion | flops 3145728 | bytes 10485772 | tf_op jit(solution)/shard_map/div | solution.py:90
  638.6 2.7 copy.56
  641.3 0.0 copy-done.1
  (3 shorter events, 0.0 us)
Async XLA Ops:
  7.2 49.4 %copy-start = (f32[8,8,2,2]{1,3,2,0:T(2,128)S(1)}, f32[8,8,2,2]{1,3,2,0:T(2,128)}, u32[]{:S(2)}) copy-start(f32[8,8,2,2]{1,3,2,0:T(2,128)} %param.10) | copy-start | bytes 3076
  7.2 137.4 %all-gather.9.cloned.1.call-start = ((), (), s32[]{:S(2)}) async-start(), calls=%async_computation.5 | async-start | bytes 17825792 | tf_op jit(solution)/shard_map/all_gather | solution.py:35
  11.7 1.4 copy-start.3
  11.7 3.5 copy-start.4
  15.2 185.8 %all-gather.5.cloned.1.call-start = ((), (), s32[]{:S(2)}) async-start(), calls=%async_computation.2 | async-start | bytes 6291456 | tf_op jit(solution)/shard_map/all_gather | solution.py:28
  17.8 352.8 %all-gather.7.cloned.1.call-start = ((), (), s32[]{:S(2)}) async-start(), calls=%async_computation.3 | async-start | bytes 35651584 | tf_op jit(solution)/shard_map/all_gather | solution.py:47
  53.6 2.7 copy-start.6
  53.6 2.8 copy-start.7
  56.3 453.2 %reduce-scatter.2.cloned.1.call-start = ((), (), s32[]{:S(2)}) async-start(), calls=%async_computation.4 | async-start | bytes 6291456 | tf_op jit(solution)/shard_map/reduce_scatter | solution.py:52
  201.0 25.6 %copy-start.5 = (f32[8,8,2,2,2,2]{1,0,5,4,3,2:T(8,128)S(1)}, f32[8,8,2,2,2,2]{1,0,5,4,3,2:T(8,128)}, u32[]{:S(2)}) copy-start(f32[8,8,2,2,2,2]{1,0,5,4,3,2:T(8,128)} %copy.48) | copy-start | bytes 12292
  509.5 43.3 %copy-start.2 = (f32[128,4,1024]{2,0,1:T(8,128)S(1)}, f32[128,4,1024]{2,0,1:T(8,128)}, u32[]{:S(2)}) copy-start(f32[128,4,1024]{2,0,1:T(8,128)} %reduce-scatter.2.cloned.1.call-done) | copy-start | bytes 6291460
  631.7 9.6 %copy-start.1 = (f32[8,8,2,2]{1,3,2,0:T(2,128)S(1)}, f32[8,8,2,2]{1,3,2,0:T(2,128)}, u32[]{:S(2)}) copy-start(f32[8,8,2,2]{1,3,2,0:T(2,128)} %param.10) | copy-start | bytes 3076
Sparse Core Ops, SparseCore 0:
  15.3 129.1 all-gather.8
  146.1 54.8 all-gather.4
  202.6 168.0 all-gather.6
  417.4 54.3 reduce-scatter.1
